TPU v7x, 32 devices: a whole 2x2x4 slice. The times are simulated.
32 devices in a mesh: seq: 8 (over z, x), head: 4 (over y, core).
Axes of the slice: x: 2, y: 2, z: 4, core: 2. Of those that a mesh axis runs over, the one named last changes fastest.
Arguments:
- video_q: bfloat16 [1024, 4096], P(('seq', 'head')), may hold values from -200 to 200
- video_k: bfloat16 [1024, 4096], P(('seq', 'head')), may hold values from -6 to 6
- video_v: bfloat16 [1024, 4096], P(('seq', 'head')), may hold values from -6 to 6
- text_k: bfloat16 [512, 4096], P(None, 'head'), may hold values from -6 to 6
- text_v: bfloat16 [512, 4096], P(None, 'head'), may hold values from -6 to 6
- out_weight: bfloat16 [4096, 5120], P('head'), may hold values from -0.09375 to 0.09375
Outputs:
- video_out: bfloat16 [1024, 5120], P(('seq', 'head'))
All inputs are finite; a program needn't handle non-finite values.
Results may differ from a plain program's by a relative error of at most 0.018.
Values may be sent and summed in bfloat16 or wider, within the bound.
A program may use at most 128 MiB of HBM per device.

v0:
```python
import jax
import jax.numpy as jnp
from jax import lax
from jax.sharding import PartitionSpec as P

HD = 128


def as_heads(array):
    return array.reshape(array.shape[0], array.shape[1] // HD, HD)


def scores_of(query_heads, key_heads):
    return jnp.einsum(
        "qhd,khd->hqk", query_heads, key_heads, preferred_element_type=jnp.float32
    ) * HD ** (-0.5)


def weigh_values(scores, row_max, value_heads):
    weights = jnp.exp(scores - row_max[..., None]).astype(jnp.bfloat16)
    totals = jnp.sum(weights.astype(jnp.float32), axis=2)
    summed = jnp.einsum("hqk,khd->hqd", weights, value_heads, preferred_element_type=jnp.float32)
    return (totals, summed)


def local_partial(query_heads, key_heads, value_heads):
    scores = scores_of(query_heads, key_heads)
    row_max = jnp.max(scores, axis=2)
    totals, summed = weigh_values(scores, row_max, value_heads)
    return (row_max, totals, summed)


def combine_partial(first, second):
    joint = jnp.maximum(first[0], second[0])
    first_factor = jnp.exp(first[0] - joint)
    second_factor = jnp.exp(second[0] - joint)
    totals = first[1] * first_factor + second[1] * second_factor
    summed = first[2] * first_factor[..., None] + second[2] * second_factor[..., None]
    return (joint, totals, summed)


def body(video_q, video_k, video_v, text_k, text_v, out_weight):
    queries, key_rows, value_rows = (
        lax.all_to_all(video_q, "head", split_axis=1, concat_axis=0, tiled=True),
        lax.all_to_all(video_k, "head", split_axis=1, concat_axis=0, tiled=True),
        lax.all_to_all(video_v, "head", split_axis=1, concat_axis=0, tiled=True),
    )
    rows_here = queries.shape[0]
    query_heads = as_heads(queries)
    text_part = local_partial(query_heads, as_heads(text_k), as_heads(text_v))
    merged = combine_partial(
        text_part,
        local_partial(
            query_heads,
            as_heads(lax.all_gather(key_rows, "seq", axis=0, tiled=True)),
            as_heads(lax.all_gather(value_rows, "seq", axis=0, tiled=True)),
        ),
    )
    normalized = merged[2] / merged[1][..., None]
    attended = normalized.transpose(1, 0, 2).reshape(rows_here, -1).astype(jnp.bfloat16)
    return lax.psum_scatter(
        jnp.dot(attended, out_weight, preferred_element_type=jnp.float32).astype(jnp.bfloat16),
        "head",
        scatter_dimension=0,
        tiled=True,
    )


def solution(mesh):
    in_specs = (
        P(("seq", "head"), None),
        P(("seq", "head"), None),
        P(("seq", "head"), None),
        P(None, "head"),
        P(None, "head"),
        P("head", None),
    )
    out_specs = P(("seq", "head"), None)
    return jax.shard_map(body, mesh=mesh, in_specs=in_specs, out_specs=out_specs, check_vma=False)
```

profile of v0, /device:TPU:0, one launch (start us, length us, event | category | flops | bytes accessed | tf_op | source)
XLA Modules:
  0.0 162.2 jit_solution(479309963512354271)
XLA Ops:
  6.5 0.0 copy-start
  6.5 0.0 copy-start.4
  6.5 0.0 copy-start.3
  6.5 0.0 all-gather.3.cloned.1.call-start
  6.5 1.1 copy.63
  7.7 10.2 %all_to_all.54 = bf16[32,4,1024]{2,0,1:T(8,128)(2,1)} all-to-all(bf16[32,4,1024]{2,0,1:T(8,128)(2,1)S(1)} %bitcast.80), channel_id=1, replica_groups=mesh['seq'=8,'head'=4] {'head'}, dimensions={1} | all-to-all | bytes 524288 | tf_op jit(solution)/shard_map/all_to_all | solution.py:45
  17.8 0.0 all-gather.3.cloned.1.call-update
  17.9 0.0 all-gather.5.cloned.1.call-start
  17.9 1.0 copy.62
  18.9 9.1 %all_to_all.55 = bf16[32,4,1024]{2,0,1:T(8,128)(2,1)} all-to-all(bf16[32,4,1024]{2,0,1:T(8,128)(2,1)S(1)} %bitcast.81), channel_id=1, replica_groups=mesh['seq'=8,'head'=4] {'head'}, dimensions={1} | all-to-all | bytes 524288 | tf_op jit(solution)/shard_map/all_to_all | solution.py:46
  28.0 0.0 all-gather.5.cloned.1.call-update
  28.0 0.0 copy-done.4
  28.0 0.7 copy.64
  28.7 3.4 %all-to-all-start = ((bf16[32,4,1024]{2,0,1:T(8,128)(2,1)}), bf16[32,4,1024]{2,0,1:T(8,128)(2,1)S(1)}, u32[]{:S(2)}, u32[]{:S(2)}) async-start(bf16[32,4,1024]{2,0,1:T(8,128)(2,1)} %bitcast.71), calls=%async_computation | async-start | bytes 524288 | tf_op jit(solution)/shard_map/all_to_all | solution.py:44
  32.1 0.0 reduce-scatter.2.cloned.1.call-start
  32.2 0.0 copy-done.3
  32.2 1.3 copy.39
  33.5 4.6 %all-to-all-done = bf16[32,4,1024]{2,0,1:T(8,128)(2,1)S(1)} async-done(((bf16[32,4,1024]{2,0,1:T(8,128)(2,1)}), bf16[32,4,1024]{2,0,1:T(8,128)(2,1)S(1)}, u32[]{:S(2)}, u32[]{:S(2)}) %all-to-all-start) | async-done | bytes 262176 | tf_op jit(solution)/shard_map/all_to_all | solution.py:44
  38.2 0.0 copy-done
  38.2 0.5 multiply_reduce_fusion.1
  38.7 0.6 convert_reduce_fusion.1
  39.3 28.5 %all-gather.3.cloned.1.call-done = bf16[1024,1024]{1,0:T(8,128)(2,1)} async-done(((bf16[128,1024]{1,0:T(8,128)(2,1)}), bf16[1024,1024]{1,0:T(8,128)(2,1)}) %all-gather.3.cloned.1.call-update) | async-done | bytes 2097168 | tf_op jit(solution)/shard_map/all_gather | solution.py:55
  67.8 3.9 %copy.33 = bf16[1024,1024]{0,1:T(8,128)(2,1)} copy(bf16[1024,1024]{1,0:T(8,128)(2,1)} %all-gather.3.cloned.1.call-done) | data formatting | bytes 4194304 | tf_op jit(solution)/shard_map/all_gather | solution.py:55
  71.7 2.4 %multiply_reduce_fusion = (f32[8,128]{1,0:T(8,128)S(1)}, f32[8,128,1024]{2,1,0:T(8,128)S(1)}) fusion(bf16[1024,8,128]{0,2,1:T(8,128)(2,1)} %bitcast.72, bf16[128,8,128]{2,1,0:T(8,128)(2,1)S(1)} %bitcast.75), kind=kOutput, calls=%fused_computation.3 | convolution fusion | flops 270531584 | bytes 6557696 | tf_op jit(solution)/shard_map/qhd,khd->hqk/dot_general | solution.py:14
  74.1 0.0 copy-start.1
  74.1 0.0 copy-start.2
  74.1 0.9 convert_reduce_fusion
  75.0 1.0 copy-done.1
  76.0 0.1 copy-done.2
  76.1 1.4 fusion
  77.5 40.0 %all-gather.5.cloned.1.call-done = bf16[1024,1024]{1,0:T(8,128)(2,1)} async-done(((bf16[128,1024]{1,0:T(8,128)(2,1)}), bf16[1024,1024]{1,0:T(8,128)(2,1)}) %all-gather.5.cloned.1.call-update) | async-done | bytes 2097168 | tf_op jit(solution)/shard_map/all_gather | solution.py:56
  117.6 2.9 %copy.37 = bf16[1024,1024]{0,1:T(8,128)(2,1)S(1)} copy(bf16[1024,1024]{1,0:T(8,128)(2,1)} %all-gather.5.cloned.1.call-done) | data formatting | bytes 4194304 | tf_op jit(solution)/shard_map/all_gather | solution.py:56
  120.4 3.4 %fusion.4 = bf16[128,8,128]{0,2,1:T(8,128)(2,1)S(1)} fusion(f32[128,8,128]{0,2,1:T(8,128)} %fusion, bf16[1024,8,128]{0,2,1:T(8,128)(2,1)S(1)} %bitcast.76, f32[8,128,1024]{2,1,0:T(8,128)} %copy-done.1, f32[8,128]{1,0:T(8,128)S(1)} %get-tuple-element.8, f32[128,8]{0,1:T(8,128)S(1)} %get-tuple-element.5, f32[128,8]{0,1:T(8,128)S(1)} %get-tuple-element.6), kind=kOutput, calls=%fused_computation.13 | convolution fusion | flops 272105472 | bytes 7090176 | tf_op jit(solution)/shard_map/hqk,khd->hqd/dot_general | solution.py:22
  123.8 6.6 %convolution_convert_fusion = bf16[128,5120]{1,0:T(8,128)(2,1)} fusion(bf16[128,1024]{0,1:T(8,128)(2,1)S(1)} %bitcast.82, bf16[1024,5120]{1,0:T(8,128)(2,1)} %param.11), kind=kOutput, calls=%fused_computation | convolution fusion | flops 1342832640 | bytes 12058624 | tf_op jit(solution)/shard_map/dot_general | solution.py:62
  130.5 0.0 reduce-scatter.2.cloned.1.call-update
  130.5 25.1 %reduce-scatter.2.cloned.1.call-done = bf16[32,5120]{1,0:T(8,128)(2,1)} async-done(((bf16[128,5120]{1,0:T(8,128)(2,1)}), bf16[32,5120]{1,0:T(8,128)(2,1)}) %reduce-scatter.2.cloned.1.call-update) | async-done | bytes 327696 | tf_op jit(solution)/shard_map/reduce_scatter | solution.py:61
  (2 shorter events, 0.1 us)
Async XLA Ops:
  6.5 31.6 %copy-start = (bf16[512,1024]{1,0:T(8,128)(2,1)S(1)}, bf16[512,1024]{1,0:T(8,128)(2,1)}, u32[]{:S(2)}) copy-start(bf16[512,1024]{1,0:T(8,128)(2,1)} %param.9) | copy-start | bytes 3145732
  6.5 21.5 %copy-start.4 = (bf16[32,4096]{1,0:T(8,128)(2,1)S(1)}, bf16[32,4096]{1,0:T(8,128)(2,1)}, u32[]{:S(2)}) copy-start(bf16[32,4096]{1,0:T(8,128)(2,1)} %param.6) | copy-start | bytes 786436
  6.5 25.7 %copy-start.3 = (bf16[512,1024]{1,0:T(8,128)(2,1)S(1)}, bf16[512,1024]{1,0:T(8,128)(2,1)}, u32[]{:S(2)}) copy-start(bf16[512,1024]{1,0:T(8,128)(2,1)} %param.10) | copy-start | bytes 3145732
  6.5 61.2 %all-gather.3.cloned.1.call-start = ((), (), s32[]{:S(2)}) async-start(), calls=%async_computation.4 | async-start | bytes 2359296 | tf_op jit(solution)/shard_map/all_gather | solution.py:55
  17.9 99.7 %all-gather.5.cloned.1.call-start = ((), (), s32[]{:S(2)}) async-start(), calls=%async_computation.5 | async-start | bytes 2359296 | tf_op jit(solution)/shard_map/all_gather | solution.py:56
  28.7 9.4 %all-to-all-start = ((bf16[32,4,1024]{2,0,1:T(8,128)(2,1)}), bf16[32,4,1024]{2,0,1:T(8,128)(2,1)S(1)}, u32[]{:S(2)}, u32[]{:S(2)}) async-start(bf16[32,4,1024]{2,0,1:T(8,128)(2,1)} %bitcast.71), calls=%async_computation | async-start | bytes 524288 | tf_op jit(solution)/shard_map/all_to_all | solution.py:44
  32.1 123.5 %reduce-scatter.2.cloned.1.call-start = ((), (), s32[]{:S(2)}) async-start(), calls=%async_computation.6 | async-start | bytes 1638400 | tf_op jit(solution)/shard_map/reduce_scatter | solution.py:61
  74.1 1.9 %copy-start.1 = (f32[8,128,1024]{2,1,0:T(8,128)}, f32[8,128,1024]{2,1,0:T(8,128)S(1)}, u32[]{:S(2)}) copy-start(f32[8,128,1024]{2,1,0:T(8,128)S(1)} %get-tuple-element.9) | copy-start | bytes 12582916
  74.1 2.0 %copy-start.2 = (bf16[512,1024]{0,1:T(8,128)(2,1)S(1)}, bf16[512,1024]{0,1:T(8,128)(2,1)}, u32[]{:S(2)}) copy-start(bf16[512,1024]{0,1:T(8,128)(2,1)} %copy.39) | copy-start | bytes 3145732
Sparse Core Ops, SparseCore 0:
  18.0 49.7 all-gather.2
  69.9 47.6 all-gather.4
  130.6 24.9 reduce-scatter.1
where the time goes:
time: 163 us; the launch traced here: 162 us
  waiting for transfers between devices  98.2 us (60%)
  blocking collectives  19.3 us (12%)
  matrix products  14.4 us (9%)
  between operations  13.2 us (8%)
  local copies, waits for them, and re-layouts  12 us (7%)
  starting transfers between devices  3.49 us (2%)
    all_gather x1, waiting for transfers between devices, body(): lax.all_gather(value_rows, 'seq', axis=0, tiled=True)  40 us
    all_gather x1, waiting for transfers between devices, body(): lax.all_gather(key_rows, 'seq', axis=0, tiled=True)  28.5 us
    reduce_scatter x1, waiting for transfers between devices, body(): lax.psum_scatter(jnp.dot(attended, out_weight, preferred_element_type=jnp...  25.1 us
    all_to_all x1, blocking collectives, body(): lax.all_to_all(video_k, 'head', split_axis=1, concat_axis=0, tiled=True)  10.2 us
    all_to_all x1, blocking collectives, body(): lax.all_to_all(video_v, 'head', split_axis=1, concat_axis=0, tiled=True)  9.08 us
    dot_general x1, matrix products, body(): jnp.dot(attended, out_weight, preferred_element_type=jnp.float32)  6.62 us
    dot_general x2, matrix products, weigh_values(): jnp.einsum('hqk,khd->hqd', weights, value_heads, preferred_element_type=j...  4.87 us
    all_to_all x1, waiting for transfers between devices, body(): lax.all_to_all(video_q, 'head', split_axis=1, concat_axis=0, tiled=True)  4.57 us
  transfers between devices with their start and end apart: 4, of which 4 were waited for; matrix products, arithmetic and copies ran while one was open for 8% of the time, Pallas kernels for 0%

commit v1 on v0

--- a/solution.py
+++ b/solution.py
@@ -4,6 +4,12 @@
 from jax.sharding import PartitionSpec as P
 
 HD = 128
+
+
+def stacked_exchange(array, name, split, join):
+    pieces = jnp.split(array, lax.axis_size(name), axis=split)
+    got = lax.all_to_all(jnp.stack(pieces), name, 0, 0)
+    return jnp.concatenate(got, axis=join)
 
 
 def as_heads(array):
@@ -43,7 +49,7 @@
     queries, key_rows, value_rows = (
         lax.all_to_all(video_q, "head", split_axis=1, concat_axis=0, tiled=True),
         lax.all_to_all(video_k, "head", split_axis=1, concat_axis=0, tiled=True),
-        lax.all_to_all(video_v, "head", split_axis=1, concat_axis=0, tiled=True),
+        stacked_exchange(video_v, "head", 1, 0),
     )
     rows_here = queries.shape[0]
     query_heads = as_heads(queries)

time: 163 us -> 161 us (0.988)
  local copies, waits for them, and re-layouts: 12 us -> 10 us
    all_gather x1 -> x0, local copies, waits for them, and re-layouts: 2.85 us -> none  [body(): lax.all_gather(value_rows, 'seq', axis=0, tiled=True)]
  transfers between devices with their start and end apart: 4 -> 4, of which waited for: 4 -> 4; matrix products, arithmetic and copies ran while one was open for 8% -> 9% of each run, Pallas kernels for 0% -> 0%
where the time goes in v1:
time: 161 us
  waiting for transfers between devices  98.8 us (61%)
  blocking collectives  18.7 us (12%)
  matrix products  15 us (9%)
  between operations  13.2 us (8%)
  local copies, waits for them, and re-layouts  10 us (6%)
  starting transfers between devices  3.49 us (2%)
    all_gather x1, waiting for transfers between devices, body(): lax.all_gather(value_rows, 'seq', axis=0, tiled=True)  41.2 us
    all_gather x1, waiting for transfers between devices, body(): lax.all_gather(key_rows, 'seq', axis=0, tiled=True)  28.3 us
    reduce_scatter x1, waiting for transfers between devices, body(): lax.psum_scatter(jnp.dot(attended, out_weight, preferred_element_type=jnp...  24.8 us
    all_to_all x1, blocking collectives, body(): lax.all_to_all(video_k, 'head', split_axis=1, concat_axis=0, tiled=True)  10.3 us
    all_to_all x1, blocking collectives, stacked_exchange(): got = lax.all_to_all(jnp.stack(pieces), name, 0, 0)  8.39 us
    dot_general x1, matrix products, body(): jnp.dot(attended, out_weight, preferred_element_type=jnp.float32)  6.62 us
    dot_general x2, matrix products, weigh_values(): jnp.einsum('hqk,khd->hqd', weights, value_heads, preferred_element_type=j...  5.45 us
    all_to_all x1, waiting for transfers between devices, body(): lax.all_to_all(video_q, 'head', split_axis=1, concat_axis=0, tiled=True)  4.58 us
  transfers between devices with their start and end apart: 4, of which 4 were waited for; matrix products, arithmetic and copies ran while one was open for 9% of the time, Pallas kernels for 0%

profile of v1, /device:TPU:0, one launch (start us, length us, event | category | flops | bytes accessed | tf_op | source)
XLA Modules:
  0.0 160.8 jit_solution(2538283910031757952)
XLA Ops:
  6.5 0.0 copy-start
  6.5 0.0 copy-start.4
  6.5 0.0 all-gather.3.cloned.1.call-start
  6.5 1.1 copy.58
  7.6 0.0 copy-start.3
  7.6 10.3 %all_to_all.40 = bf16[32,4,1024]{2,0,1:T(8,128)(2,1)} all-to-all(bf16[32,4,1024]{2,0,1:T(8,128)(2,1)S(1)} %bitcast.81), channel_id=1, replica_groups=mesh['seq'=8,'head'=4] {'head'}, dimensions={1} | all-to-all | bytes 524288 | tf_op jit(solution)/shard_map/all_to_all | solution.py:51
  17.9 0.0 all-gather.3.cloned.1.call-update
  18.0 0.0 all-gather.5.cloned.1.call-start
  18.0 1.0 slice_bitcast_fusion.3
  19.0 8.4 %all_to_all.41 = bf16[4,32,1024]{2,1,0:T(8,128)(2,1)S(1)} all-to-all(bf16[4,32,1024]{2,1,0:T(8,128)(2,1)S(1)} %pad_maximum_fusion), channel_id=1, replica_groups=mesh['seq'=8,'head'=4] {'head'}, dimensions={0} | all-to-all | bytes 524288 | tf_op jit(solution)/shard_map/all_to_all | solution.py:11
  27.4 0.8 copy.35
  28.2 0.0 all-gather.5.cloned.1.call-update
  28.3 0.0 copy-done.4
  28.3 0.7 copy.59
  29.0 3.4 %all-to-all-start = ((bf16[32,4,1024]{2,0,1:T(8,128)(2,1)}), bf16[32,4,1024]{2,0,1:T(8,128)(2,1)S(1)}, u32[]{:S(2)}, u32[]{:S(2)}) async-start(bf16[32,4,1024]{2,0,1:T(8,128)(2,1)} %bitcast.73), calls=%async_computation | async-start | bytes 524288 | tf_op jit(solution)/shard_map/all_to_all | solution.py:50
  32.4 0.0 reduce-scatter.2.cloned.1.call-start
  32.5 0.0 copy-done.3
  32.5 1.3 copy.37
  33.8 4.6 %all-to-all-done = bf16[32,4,1024]{2,0,1:T(8,128)(2,1)S(1)} async-done(((bf16[32,4,1024]{2,0,1:T(8,128)(2,1)}), bf16[32,4,1024]{2,0,1:T(8,128)(2,1)S(1)}, u32[]{:S(2)}, u32[]{:S(2)}) %all-to-all-start) | async-done | bytes 262176 | tf_op jit(solution)/shard_map/all_to_all | solution.py:50
  38.4 0.0 copy-done
  38.5 0.5 multiply_reduce_fusion.1
  39.0 0.6 convert_reduce_fusion.1
  39.6 28.3 %all-gather.3.cloned.1.call-done = bf16[1024,1024]{1,0:T(8,128)(2,1)} async-done(((bf16[128,1024]{1,0:T(8,128)(2,1)}), bf16[1024,1024]{1,0:T(8,128)(2,1)}) %all-gather.3.cloned.1.call-update) | async-done | bytes 2097168 | tf_op jit(solution)/shard_map/all_gather | solution.py:61
  67.9 3.9 %copy.32 = bf16[1024,1024]{0,1:T(8,128)(2,1)} copy(bf16[1024,1024]{1,0:T(8,128)(2,1)} %all-gather.3.cloned.1.call-done) | data formatting | bytes 4194304 | tf_op jit(solution)/shard_map/all_gather | solution.py:61
  71.8 2.4 %multiply_reduce_fusion = (f32[8,128]{1,0:T(8,128)S(1)}, f32[8,128,1024]{2,1,0:T(8,128)S(1)}) fusion(bf16[1024,8,128]{0,2,1:T(8,128)(2,1)} %bitcast.74, bf16[128,8,128]{2,1,0:T(8,128)(2,1)S(1)} %bitcast.77), kind=kOutput, calls=%fused_computation.3 | convolution fusion | flops 270531584 | bytes 6557696 | tf_op jit(solution)/shard_map/qhd,khd->hqk/dot_general | solution.py:20
  74.2 0.0 copy-start.1
  74.2 0.0 copy-start.2
  74.2 0.9 convert_reduce_fusion
  75.1 1.0 copy-done.1
  76.1 0.1 copy-done.2
  76.2 1.4 fusion
  77.6 41.2 %all-gather.5.cloned.1.call-done = bf16[1024,1024]{0,1:T(8,128)(2,1)} async-done(((bf16[128,1024]{0,1:T(8,128)(2,1)}), bf16[1024,1024]{0,1:T(8,128)(2,1)}) %all-gather.5.cloned.1.call-update) | async-done | bytes 2097168 | tf_op jit(solution)/shard_map/all_gather | solution.py:62
  118.8 4.0 %fusion.4 = bf16[128,8,128]{0,2,1:T(8,128)(2,1)S(1)} fusion(f32[128,8,128]{0,2,1:T(8,128)} %fusion, bf16[1024,8,128]{0,2,1:T(8,128)(2,1)} %bitcast.85, f32[8,128,1024]{2,1,0:T(8,128)} %copy-done.1, f32[8,128]{1,0:T(8,128)S(1)} %get-tuple-element.12, f32[128,8]{0,1:T(8,128)S(1)} %get-tuple-element.5, f32[128,8]{0,1:T(8,128)S(1)} %get-tuple-element.6), kind=kOutput, calls=%fused_computation.13 | convolution fusion | flops 272105472 | bytes 7090176 | tf_op jit(solution)/shard_map/hqk,khd->hqd/dot_general | solution.py:28
  122.8 6.6 %convolution_convert_fusion = bf16[128,5120]{1,0:T(8,128)(2,1)} fusion(bf16[128,1024]{0,1:T(8,128)(2,1)S(1)} %bitcast.82, bf16[1024,5120]{1,0:T(8,128)(2,1)} %param.11), kind=kOutput, calls=%fused_computation | convolution fusion | flops 1342832640 | bytes 12058624 | tf_op jit(solution)/shard_map/dot_general | solution.py:68
  129.4 0.0 reduce-scatter.2.cloned.1.call-update
  129.5 24.8 %reduce-scatter.2.cloned.1.call-done = bf16[32,5120]{1,0:T(8,128)(2,1)} async-done(((bf16[128,5120]{1,0:T(8,128)(2,1)}), bf16[32,5120]{1,0:T(8,128)(2,1)}) %reduce-scatter.2.cloned.1.call-update) | async-done | bytes 327696 | tf_op jit(solution)/shard_map/reduce_scatter | solution.py:67
  (3 shorter events, 0.1 us)
Async XLA Ops:
  6.5 31.9 %copy-start = (bf16[512,1024]{1,0:T(8,128)(2,1)S(1)}, bf16[512,1024]{1,0:T(8,128)(2,1)}, u32[]{:S(2)}) copy-start(bf16[512,1024]{1,0:T(8,128)(2,1)} %param.9) | copy-start | bytes 3145732
  6.5 21.7 %copy-start.4 = (bf16[32,4096]{1,0:T(8,128)(2,1)S(1)}, bf16[32,4096]{1,0:T(8,128)(2,1)}, u32[]{:S(2)}) copy-start(bf16[32,4096]{1,0:T(8,128)(2,1)} %param.6) | copy-start | bytes 786436
  6.5 61.3 %all-gather.3.cloned.1.call-start = ((), (), s32[]{:S(2)}) async-start(), calls=%async_computation.4 | async-start | bytes 2359296 | tf_op jit(solution)/shard_map/all_gather | solution.py:61
  7.6 24.9 %copy-start.3 = (bf16[512,1024]{1,0:T(8,128)(2,1)S(1)}, bf16[512,1024]{1,0:T(8,128)(2,1)}, u32[]{:S(2)}) copy-start(bf16[512,1024]{1,0:T(8,128)(2,1)} %param.10) | copy-start | bytes 3145732
  18.0 100.8 %all-gather.5.cloned.1.call-start = ((), (), s32[]{:S(2)}) async-start(), calls=%async_computation.5 | async-start | bytes 2359296 | tf_op jit(solution)/shard_map/all_gather | solution.py:62
  29.0 9.4 %all-to-all-start = ((bf16[32,4,1024]{2,0,1:T(8,128)(2,1)}), bf16[32,4,1024]{2,0,1:T(8,128)(2,1)S(1)}, u32[]{:S(2)}, u32[]{:S(2)}) async-start(bf16[32,4,1024]{2,0,1:T(8,128)(2,1)} %bitcast.73), calls=%async_computation | async-start | bytes 524288 | tf_op jit(solution)/shard_map/all_to_all | solution.py:50
  32.4 121.8 %reduce-scatter.2.cloned.1.call-start = ((), (), s32[]{:S(2)}) async-start(), calls=%async_computation.6 | async-start | bytes 1638400 | tf_op jit(solution)/shard_map/reduce_scatter | solution.py:67
  74.2 1.9 %copy-start.1 = (f32[8,128,1024]{2,1,0:T(8,128)}, f32[8,128,1024]{2,1,0:T(8,128)S(1)}, u32[]{:S(2)}) copy-start(f32[8,128,1024]{2,1,0:T(8,128)S(1)} %get-tuple-element.13) | copy-start | bytes 12582916
  74.2 2.0 %copy-start.2 = (bf16[512,1024]{0,1:T(8,128)(2,1)S(1)}, bf16[512,1024]{0,1:T(8,128)(2,1)}, u32[]{:S(2)}) copy-start(bf16[512,1024]{0,1:T(8,128)(2,1)} %copy.37) | copy-start | bytes 3145732
Sparse Core Ops, SparseCore 0:
  18.1 49.7 all-gather.2
  69.9 48.8 all-gather.4
  129.6 24.5 reduce-scatter.1
